TPU v7x, 128 devices: a whole 4x4x4 slice. The times are simulated.
128 devices in a mesh: gx: 8 (over z, core), gy: 16 (over y, x).
Axes of the slice: x: 4, y: 4, z: 4, core: 2. Of those that a mesh axis runs over, the one named last changes fastest.
Arguments:
- particles: bfloat16 [64, 256, 64, 256], P('gx', 'gy'), may hold values from -6 to 6
- bias: float32 [64, 256, 64], P('gx', 'gy'), may hold values from -4 to 4
- spread: float32 [64, 256], P('gx', 'gy'), may hold values from 128 to 512
- precision: bfloat16 [64, 64], replicated, may hold values from -1 to 1
- coupling_h: bfloat16 [64, 64], replicated, may hold values from -0.059814453 to 0.059814453
- coupling_v: bfloat16 [64, 64], replicated, may hold values from -0.059814453 to 0.059814453
Outputs:
- force: bfloat16 [64, 256, 64, 256], P('gx', 'gy')
- stein: float32 [], replicated
All inputs are finite; a program needn't handle non-finite values.
Results may differ from a plain program's by a relative error of at most 0.0029.
Values may be sent and summed in bfloat16 or wider, within the bound.
A program may use at most 384 MiB of HBM per device.

v0:
```python
import functools

import jax
import jax.numpy as jnp
from jax import lax
from jax.sharding import Mesh
from jax.sharding import PartitionSpec as P

GX_GY = ("gx_0", "gx_1", "gy_0", "gy_1")
GX = ("gx_0", "gx_1")
GY = ("gy_0", "gy_1")


def with_halo(cells, sides, width):
    for axis, dim in sides:
        count = lax.axis_size(axis)
        ends = count - 1
        head = lax.slice_in_dim(cells, 0, width, axis=dim)
        tail = lax.slice_in_dim(cells, cells.shape[dim] - width, cells.shape[dim], axis=dim)
        cells = jnp.concatenate(
            [
                lax.ppermute(tail, axis, [(i, (i + 1) % count) for i in range(ends)]),
                cells,
                lax.ppermute(head, axis, [((i + 1) % count, i) for i in range(ends)]),
            ],
            axis=dim,
        )
    return cells


def by_axis(x, axes):
    return functools.reduce(lax.psum, axes, x)


def distances(states):
    values = states.astype(jnp.float32)
    squares = jnp.sum(values * values, axis=-2)
    inner_prod = jnp.einsum("rcdp,rcdq->rcpq", states, states, preferred_element_type=jnp.float32)
    return squares[..., :, None] + squares[..., None, :] - 2.0 * inner_prod


def mixing(matrix, states):
    return jnp.einsum("ed,rcdp->rcep", matrix, states, preferred_element_type=jnp.float32)


def mixing_t(matrix, states):
    return jnp.einsum("de,rcdp->rcep", matrix, states, preferred_element_type=jnp.float32)


def on_device(particles, bias, spread, precision, coupling_h, coupling_v):
    tile_rows, tile_cols, state_size, particle_count = particles.shape
    padded = with_halo(particles, ((GX, 0), (GY, 1)), 1)
    own_dist = distances(particles)
    upper_rim = distances(padded[:1, 1:-1])[0]
    lower_rim = distances(padded[-1:, 1:-1])[0]
    left_rim = distances(padded[1:-1, :1])[:, 0]
    right_rim = distances(padded[1:-1, -1:])[:, 0]
    blanket = (
        own_dist
        + jnp.concatenate([upper_rim[None], own_dist[:-1]], axis=0)
        + jnp.concatenate([own_dist[1:], lower_rim[None]], axis=0)
        + jnp.concatenate([left_rim[:, None], own_dist[:, :-1]], axis=1)
        + jnp.concatenate([own_dist[:, 1:], right_rim[:, None]], axis=1)
    )
    scores = (
        -mixing(precision, particles)
        + bias[..., None]
        + mixing(coupling_h, padded[1:-1, 2:])
        + mixing_t(coupling_h, padded[1:-1, :-2])
        + mixing(coupling_v, padded[2:, 1:-1])
        + mixing_t(coupling_v, padded[:-2, 1:-1])
    )
    band_width = spread[..., None, None]
    kernel = jnp.exp(-blanket / band_width)
    kernel_low = kernel.astype(jnp.bfloat16)
    score_low = scores.astype(jnp.bfloat16)
    colsum = jnp.sum(kernel, axis=-2)
    rowsum = jnp.sum(kernel, axis=-1)
    stacked = jnp.concatenate([score_low, particles], axis=2)
    products = jnp.einsum(
        "rcej,rcji->rcei", stacked, kernel_low, preferred_element_type=jnp.float32
    )
    pull_sum = products[:, :, :state_size]
    push_sum = products[:, :, state_size:]
    states_f = particles.astype(jnp.float32)
    score_f = score_low.astype(jnp.float32)
    inverse_width = 2.0 / band_width
    force = (pull_sum - inverse_width * (push_sum - states_f * colsum[:, :, None, :])).astype(
        jnp.bfloat16
    )
    self_dots = jnp.sum(states_f * score_f, axis=-2)
    factor = 2.0 / spread
    cross_terms = jnp.sum(score_f * pull_sum, axis=(-2, -1)) + factor * (
        jnp.sum(rowsum * self_dots, axis=-1)
        - jnp.sum(states_f * pull_sum, axis=(-2, -1))
        - jnp.sum(score_f * push_sum, axis=(-2, -1))
        + jnp.sum(colsum * self_dots, axis=-1)
    )
    trace_terms = jnp.sum(kernel, axis=(-2, -1)) * (2.0 * state_size) / spread - 4.0 / (
        spread * spread
    ) * jnp.sum(kernel * own_dist, axis=(-2, -1))
    local_sum = jnp.sum(cross_terms + trace_terms)
    stein_sum = by_axis(local_sum, GX_GY)
    node_pairs = (
        tile_rows
        * lax.axis_size(GX)
        * tile_cols
        * lax.axis_size(GY)
        * particle_count
        * particle_count
    )
    return (force, stein_sum / node_pairs)


def solution(mesh):
    torus = Mesh(mesh.devices.reshape(4, 2, 4, 4), ("gx_0", "gx_1", "gy_0", "gy_1"))
    in_specs = (P(GX, GY, None, None), P(GX, GY, None), P(GX, GY), P(), P(), P())
    out_specs = (P(GX, GY, None, None), P())
    return jax.shard_map(
        on_device, mesh=torus, in_specs=in_specs, out_specs=out_specs, check_vma=False
    )
```

profile of v0, /device:TPU:1, one launch (start us, length us, event | category | flops | bytes accessed | tf_op | source)
XLA Modules:
  0.0 281.3 jit_solution(4346571886331762511)
XLA Ops:
  0.7 1.4 fusion.57
  2.1 3.4 %collective-permute-start.1 = (bf16[1,16,64,256]{3,2,1,0:T(8,128)(2,1)S(1)}, bf16[1,16,64,256]{3,2,1,0:T(8,128)(2,1)S(1)}, u32[]{:S(2)}, u32[]{:S(2)}) collective-permute-start(bf16[1,16,64,256]{3,2,1,0:T(8,128)(2,1)S(1)} %get-tuple-element.20), channel_id=1, source_target_pairs={{16,0},{32,16},{48,32},{64,48},{80,64},{96,80},{112,96},{17,1},{33... | collective-permute-start | bytes 1572872 | tf_op jit(solution)/shard_map/ppermute | solution.py:24
  5.5 3.6 %collective-permute-start = (bf16[1,16,64,256]{3,2,1,0:T(8,128)(2,1)S(1)}, bf16[1,16,64,256]{3,2,1,0:T(8,128)(2,1)S(1)}, u32[]{:S(2)}, u32[]{:S(2)}) collective-permute-start(bf16[1,16,64,256]{3,2,1,0:T(8,128)(2,1)S(1)} %get-tuple-element.21), channel_id=1, source_target_pairs={{0,16},{16,32},{32,48},{48,64},{64,80},{80,96},{96,112},{1,17},{17... | collective-permute-start | bytes 1572872 | tf_op jit(solution)/shard_map/ppermute | solution.py:22
  9.1 3.7 %fusion.10 = f32[8,16,256]{2,1,0:T(8,128)S(1)} fusion(bf16[8,16,64,256]{3,2,1,0:T(8,128)(2,1)} %param.6), kind=kLoop, calls=%fused_computation.19 | loop fusion | flops 6258688 | bytes 4325376 | tf_op jit(solution)/shard_map/reduce_sum | solution.py:37
  12.8 12.9 %multiply_subtract_fusion = f32[8,16,256,256]{3,2,1,0:T(8,128)} fusion(f32[8,16,256]{2,1,0:T(8,128)S(1)} %fusion.10, bf16[8,16,64,256]{3,2,1,0:T(8,128)(2,1)S(1)} %copy-done.1), kind=kOutput, calls=%fused_computation.8 | convolution fusion | flops 1098907648 | bytes 37879808 | tf_op jit(solution)/shard_map/rcdp,rcdq->rcpq/dot_general | solution.py:38
  25.7 40.8 %fusion.55 = (f32[8,15,256,256]{3,2,1,0:T(8,128)}, f32[8,15,256,256]{3,2,1,0:T(8,128)}) fusion(f32[8,16,256,256]{3,2,1,0:T(8,128)} %multiply_subtract_fusion), kind=kLoop, calls=%fused_computation.79 | loop fusion | bytes 125829120 | tf_op jit(solution)/shard_map/slice | solution.py:62
  66.4 39.5 %fusion.54 = (f32[7,16,256,256]{3,2,1,0:T(8,128)}, f32[7,16,256,256]{3,2,1,0:T(8,128)}) fusion(f32[8,16,256,256]{3,2,1,0:T(8,128)} %multiply_subtract_fusion), kind=kLoop, calls=%fused_computation.78 | loop fusion | bytes 117440512 | tf_op jit(solution)/shard_map/slice | solution.py:60
  106.0 4.5 %fusion.45 = f32[8,16,256,64]{2,3,1,0:T(8,128)} fusion(bf16[8,16,64,256]{3,2,1,0:T(8,128)(2,1)S(1)} %copy-done.1, bf16[64,64]{1,0:T(8,128)(2,1)S(1)} %copy-done.8), kind=kOutput, calls=%fused_computation.65 | convolution fusion | flops 268435456 | bytes 12591104 | tf_op jit(solution)/shard_map/ed,rcdp->rcep/dot_general | solution.py:43
  110.5 0.3 constant_dynamic-update-slice_fusion.1
  110.9 3.1 %collective-permute-start.3 = (bf16[10,1,64,256]{3,2,1,0:T(8,128)(2,1)S(1)}, bf16[10,1,64,256]{3,2,1,0:T(8,128)(2,1)S(1)}, u32[]{:S(2)}, u32[]{:S(2)}) collective-permute-start(bf16[10,1,64,256]{3,2,1,0:T(8,128)(2,1)S(1)} %get-tuple-element.18), channel_id=1, source_target_pairs={{0,1},{1,2},{2,3},{3,4},{4,5},{5,6},{6,7},{7,8},{8,9},{9,10},{10,1... | collective-permute-start | bytes 983048 | tf_op jit(solution)/shard_map/ppermute | solution.py:22
  114.1 1.3 collective-permute-start.2
  115.4 0.1 multiply_reduce_fusion.1
  115.5 4.5 %fusion.29 = f32[8,16,256,64]{2,3,1,0:T(8,128)} fusion(bf16[1,16,64,256]{3,2,1,0:T(8,128)(2,1)S(1)} %collective-permute-done.1, bf16[8,16,64,256]{3,2,1,0:T(8,128)(2,1)S(1)} %copy-done.1, bf16[64,64]{1,0:T(8,128)(2,1)S(1)} %copy-done.6), kind=kOutput, calls=%fused_computation.40 | convolution fusion | flops 276824064 | bytes 13115392 | tf_op jit(solution)/shard_map/ed,rcdp->rcep/dot_general | solution.py:43
  120.0 2.5 subtract_bitcast_fusion
  122.6 0.1 multiply_reduce_fusion.2
  122.7 2.6 subtract_bitcast_fusion.1
  125.3 0.1 multiply_reduce_fusion.3
  125.4 0.8 subtract_bitcast_fusion.2
  126.2 0.1 multiply_reduce_fusion.4
  126.2 1.8 subtract_bitcast_fusion.3
  128.1 60.5 %fusion.52 = (f32[8,16,256]{2,1,0:T(8,128)}, f32[8,16]{1,0:T(8,128)S(1)}, f32[8,16]{1,0:T(8,128)S(1)}, f32[8,16,256]{2,1,0:T(8,128)}, bf16[8,16,256,256]{3,2,1,0:T(8,128)(2,1)}) fusion(f32[8,16,256,256]{3,2,1,0:T(8,128)} %multiply_subtract_fusion, f32[8,16]{1,0:T(8,128)S(1)} %copy-done.7, f32[8,1,256,256]{3,2,1,0:T(8,128)S(1)} %subtract_bitcast_fusion.2, ...), kind=kLoop, calls=%fused_computation.77 | loop fusion | flops 134151936 | bytes 184813056 | tf_op jit(solution)/shard_map/reduce_sum | solution.py:78
  188.6 6.6 %fusion.20 = f32[8,16,256,64]{2,3,1,0:T(8,128)} fusion(bf16[10,16,64,256]{3,2,1,0:T(8,128)(2,1)} %copy-done.3, bf16[10,1,64,256]{3,2,1,0:T(8,128)(2,1)S(1)} %collective-permute-done.3, bf16[64,64]{1,0:T(8,128)(2,1)S(1)} %copy-done), kind=kOutput, calls=%fused_computation.30 | convolution fusion | flops 279576576 | bytes 13967360 | tf_op jit(solution)/shard_map/de,rcdp->rcep/dot_general | solution.py:47
  195.2 6.7 %fusion.31 = f32[8,16,256,64]{2,3,1,0:T(8,128)} fusion(bf16[10,1,64,256]{3,2,1,0:T(8,128)(2,1)S(1)} %collective-permute-done.2, bf16[10,16,64,256]{3,2,1,0:T(8,128)(2,1)} %copy-done.3, bf16[64,64]{1,0:T(8,128)(2,1)S(1)} %copy-done), kind=kOutput, calls=%fused_computation.43 | convolution fusion | flops 276824064 | bytes 13967360 | tf_op jit(solution)/shard_map/ed,rcdp->rcep/dot_general | solution.py:43
  201.9 14.7 %fusion.28 = bf16[8,16,64,256]{3,2,1,0:T(8,128)(2,1)} fusion(f32[8,16,256,64]{2,3,1,0:T(8,128)} %fusion.29, f32[8,16,256,64]{2,3,1,0:T(8,128)} %fusion.20, f32[8,16,256,64]{2,3,1,0:T(8,128)} %fusion.31, f32[8,16,256,64]{2,3,1,0:T(8,128)} %fusion.45, f32[8,16,64]{2,1,0:T(8,128)} %param.7, bf16[8,16,64,256]{3,2,1,0:T(8,128)(2,1)S(1)} %copy-done.2, ...), kind=kOutput, calls=%fused_computation.38 | convolution fusion | flops 292552704 | bytes 42508288 | tf_op jit(solution)/shard_map/de,rcdp->rcep/dot_general | solution.py:47
  216.6 15.8 %fusion.6 = f32[8,16,128,256]{3,2,1,0:T(8,128)} fusion(bf16[8,16,256,256]{3,2,1,0:T(8,128)(2,1)} %get-tuple-element.12, bf16[8,16,64,256]{3,2,1,0:T(8,128)(2,1)} %param.6, bf16[8,16,64,256]{3,2,1,0:T(8,128)(2,1)} %fusion.28), kind=kOutput, calls=%fused_computation.9 | convolution fusion | flops 2164260864 | bytes 41943040 | tf_op jit(solution)/shard_map/rcej,rcji->rcei/dot_general | solution.py:80
  232.4 12.5 %fusion.9 = (f32[8,16]{1,0:T(8,128)S(1)}, f32[8,16]{1,0:T(8,128)S(1)}, f32[8,16]{1,0:T(8,128)S(1)}, f32[8,16,256]{2,1,0:T(8,128)S(1)}, bf16[8,16,64,256]{3,2,1,0:T(8,128)(2,1)}) fusion(bf16[8,16,64,256]{3,2,1,0:T(8,128)(2,1)} %fusion.28, f32[8,16,128,256]{3,2,1,0:T(8,128)} %fusion.6, bf16[8,16,64,256]{3,2,1,0:T(8,128)(2,1)} %param.6, ...), kind=kLoop, calls=%fused_computation.18 | loop fusion | flops 31424128 | bytes 29624320 | tf_op jit(solution)/shard_map/reduce_sum | solution.py:96
  244.9 0.1 multiply_reduce_fusion.6
  245.0 0.6 add_reduce_fusion
  245.6 8.2 %psum.28 = f32[]{:T(128)} all-reduce(f32[]{:T(128)} %add_reduce_fusion), channel_id=1, replica_groups=mesh['gx_0'=4,'gx_1'=2,'gy_0'=4,'gy_1'=4] {'gx_0'}, use_global_device_ids=true, to_apply=%region_16.0 | all-reduce | flops 1 | bytes 8 | tf_op jit(solution)/shard_map/psum | solution.py:32
  253.9 6.2 %psum.29 = f32[]{:T(128)} all-reduce(f32[]{:T(128)} %psum.28), channel_id=1, replica_groups=mesh['gx_0'=4,'gx_1'=2,'gy_0'=4,'gy_1'=4] {'gx_1'}, use_global_device_ids=true, to_apply=%region_17.0 | all-reduce | flops 1 | bytes 8 | tf_op jit(solution)/shard_map/psum | solution.py:32
  260.0 12.6 %psum.30 = f32[]{:T(128)} all-reduce(f32[]{:T(128)} %psum.29), channel_id=1, replica_groups=mesh['gx_0'=4,'gx_1'=2,'gy_0'=4,'gy_1'=4] {'gy_0'}, use_global_device_ids=true, to_apply=%region_18.0 | all-reduce | flops 1 | bytes 8 | tf_op jit(solution)/shard_map/psum | solution.py:32
  272.6 7.0 %psum.31 = f32[]{:T(128)} all-reduce(f32[]{:T(128)} %psum.30), channel_id=1, replica_groups=mesh['gx_0'=4,'gx_1'=2,'gy_0'=4,'gy_1'=4] {'gy_1'}, use_global_device_ids=true, to_apply=%region_19.0 | all-reduce | flops 1 | bytes 8 | tf_op jit(solution)/shard_map/psum | solution.py:32
  (26 shorter events, 0.2 us)
Async XLA Ops:
  0.6 188.0 %copy-start = (bf16[64,64]{1,0:T(8,128)(2,1)S(1)}, bf16[64,64]{1,0:T(8,128)(2,1)}, u32[]{:S(2)}) copy-start(bf16[64,64]{1,0:T(8,128)(2,1)} %param.10) | copy-start | bytes 24580
  0.6 12.1 %copy-start.1 = (bf16[8,16,64,256]{3,2,1,0:T(8,128)(2,1)S(1)}, bf16[8,16,64,256]{3,2,1,0:T(8,128)(2,1)}, u32[]{:S(2)}) copy-start(bf16[8,16,64,256]{3,2,1,0:T(8,128)(2,1)} %param.6) | copy-start | bytes 12582916
  2.1 108.7 %collective-permute-start.1 = (bf16[1,16,64,256]{3,2,1,0:T(8,128)(2,1)S(1)}, bf16[1,16,64,256]{3,2,1,0:T(8,128)(2,1)S(1)}, u32[]{:S(2)}, u32[]{:S(2)}) collective-permute-start(bf16[1,16,64,256]{3,2,1,0:T(8,128)(2,1)S(1)} %get-tuple-element.20), channel_id=1, source_target_pairs={{16,0},{32,16},{48,32},{64,48},{80,64},{96,80},{112,96},{17,1},{33... | collective-permute-start | bytes 1572872 | tf_op jit(solution)/shard_map/ppermute | solution.py:24
  5.5 104.9 %collective-permute-start = (bf16[1,16,64,256]{3,2,1,0:T(8,128)(2,1)S(1)}, bf16[1,16,64,256]{3,2,1,0:T(8,128)(2,1)S(1)}, u32[]{:S(2)}, u32[]{:S(2)}) collective-permute-start(bf16[1,16,64,256]{3,2,1,0:T(8,128)(2,1)S(1)} %get-tuple-element.21), channel_id=1, source_target_pairs={{0,16},{16,32},{32,48},{48,64},{64,80},{80,96},{96,112},{1,17},{17... | collective-permute-start | bytes 1572872 | tf_op jit(solution)/shard_map/ppermute | solution.py:22
  66.4 39.5 %copy-start.8 = (bf16[64,64]{1,0:T(8,128)(2,1)S(1)}, bf16[64,64]{1,0:T(8,128)(2,1)}, u32[]{:S(2)}) copy-start(bf16[64,64]{1,0:T(8,128)(2,1)} %param.9) | copy-start | bytes 24580
  106.0 4.5 %copy-start.7 = (f32[8,16]{1,0:T(8,128)S(1)}, f32[8,16]{1,0:T(8,128)}, u32[]{:S(2)}) copy-start(f32[8,16]{1,0:T(8,128)} %param.8) | copy-start | bytes 1540
  110.4 5.1 %copy-start.6 = (bf16[64,64]{1,0:T(8,128)(2,1)S(1)}, bf16[64,64]{1,0:T(8,128)(2,1)}, u32[]{:S(2)}) copy-start(bf16[64,64]{1,0:T(8,128)(2,1)} %param.11) | copy-start | bytes 24580
  110.9 11.7 %copy-start.3 = (bf16[10,16,64,256]{3,2,1,0:T(8,128)(2,1)}, bf16[10,16,64,256]{3,2,1,0:T(8,128)(2,1)S(1)}, u32[]{:S(2)}) copy-start(bf16[10,16,64,256]{3,2,1,0:T(8,128)(2,1)S(1)} %constant_dynamic-update-slice_fusion) | copy-start | bytes 15728644
  110.9 15.2 %collective-permute-start.3 = (bf16[10,1,64,256]{3,2,1,0:T(8,128)(2,1)S(1)}, bf16[10,1,64,256]{3,2,1,0:T(8,128)(2,1)S(1)}, u32[]{:S(2)}, u32[]{:S(2)}) collective-permute-start(bf16[10,1,64,256]{3,2,1,0:T(8,128)(2,1)S(1)} %get-tuple-element.18), channel_id=1, source_target_pairs={{0,1},{1,2},{2,3},{3,4},{4,5},{5,6},{6,7},{7,8},{8,9},{9,10},{10,1... | collective-permute-start | bytes 983048 | tf_op jit(solution)/shard_map/ppermute | solution.py:22
  114.1 11.2 %collective-permute-start.2 = (bf16[10,1,64,256]{3,2,1,0:T(8,128)(2,1)S(1)}, bf16[10,1,64,256]{3,2,1,0:T(8,128)(2,1)S(1)}, u32[]{:S(2)}, u32[]{:S(2)}) collective-permute-start(bf16[10,1,64,256]{3,2,1,0:T(8,128)(2,1)S(1)} %get-tuple-element.19), channel_id=1, source_target_pairs={{1,0},{2,1},{3,2},{4,3},{5,4},{6,5},{7,6},{8,7},{9,8},{10,9},{11,1... | collective-permute-start | bytes 983048 | tf_op jit(solution)/shard_map/ppermute | solution.py:24
  195.2 6.7 %copy-start.2 = (bf16[8,16,64,256]{3,2,1,0:T(8,128)(2,1)S(1)}, bf16[8,16,64,256]{3,2,1,0:T(8,128)(2,1)}, u32[]{:S(2)}) copy-start(bf16[8,16,64,256]{3,2,1,0:T(8,128)(2,1)} %param.6) | copy-start | bytes 12582916
  216.6 15.8 %copy-start.4 = (f32[8,16,256]{2,1,0:T(8,128)S(1)}, f32[8,16,256]{2,1,0:T(8,128)}, u32[]{:S(2)}) copy-start(f32[8,16,256]{2,1,0:T(8,128)} %get-tuple-element.5) | copy-start | bytes 393220
  232.4 12.5 %copy-start.5 = (f32[8,16,256]{2,1,0:T(8,128)S(1)}, f32[8,16,256]{2,1,0:T(8,128)}, u32[]{:S(2)}) copy-start(f32[8,16,256]{2,1,0:T(8,128)} %get-tuple-element.2) | copy-start | bytes 393220
where the time goes:
time: 285 us; the launch traced here: 281 us
  local copies, waits for them, and re-layouts  82.2 us (29%)
  other arithmetic  77.8 us (27%)
  matrix products  73.4 us (26%)
  blocking collectives  33.9 us (12%)
  starting transfers between devices  11.4 us (4%)
    reduce_sum x1, other arithmetic, on_device(): rowsum = jnp.sum(kernel, axis=-1)  60.5 us
    slice x1, local copies, waits for them, and re-layouts, on_device(): own_dist[:, :-1]  40.8 us
    slice x1, local copies, waits for them, and re-layouts, on_device(): own_dist[:-1]  39.5 us
    psum x4, blocking collectives, by_axis(): return functools.reduce(lax.psum, axes, x)  33.9 us
    dot_general x2, matrix products, mixing_t(): jnp.einsum('de,rcdp->rcep', matrix, states, preferred_element_type=jnp.fl...  21.3 us
    dot_general x5, matrix products, distances(): jnp.einsum('rcdp,rcdq->rcpq', states, states, preferred_element_type=jnp....  20.6 us
    dot_general x1, matrix products, on_device(): jnp.einsum('rcej,rcji->rcei', stacked, kernel_low, preferred_element_type...  15.8 us
    dot_general x3, matrix products, mixing(): jnp.einsum('ed,rcdp->rcep', matrix, states, preferred_element_type=jnp.fl...  15.7 us
  transfers between devices with their start and end apart: 4, of which 0 were waited for; matrix products, arithmetic and copies ran while one was open for 40% of the time, Pallas kernels for 0%

commit v1 on v0

v1 whole, which is shorter than its diff:
```python
import functools
import math

import jax
import jax.numpy as jnp
from jax import lax
from jax.experimental import pallas as pl
from jax.experimental.pallas import tpu as pltpu
from jax.sharding import PartitionSpec as P

MESH = pl.DeviceIdType.MESH
F32 = jnp.float32
BF16 = jnp.bfloat16
LOG2E = math.log2(math.e)


def row_fold(values):
    parts = [values[8 * i : 8 * i + 8] for i in range(values.shape[0] // 8)]
    while len(parts) > 1:
        parts = [a + b for a, b in zip(parts[::2], parts[1::2])]
    return parts[0]


def replicated_sum(values):
    folded = row_fold(values)
    return jnp.broadcast_to(jnp.sum(folded, axis=0, keepdims=True), folded.shape)


def top_bits(values):
    scaled = values * 65537.0
    return scaled - (scaled - values)


def split3(values):
    first = top_bits(values)
    rest = values - first
    second = top_bits(rest)
    return first, second, rest - second


class Kernel:
    def __init__(self, n_gx, n_gy, rows, cols):
        self.n_gx, self.n_gy, self.rows, self.cols = n_gx, n_gy, rows, cols
        self.brows, self.bcols = rows // 2, cols // 2

    def block_of(self, k):
        br, bc = self.brows, self.bcols
        inner = (br - 2) * (bc - 2)
        k1 = k - inner
        k2 = k1 - 2 * (bc - 2)
        k3 = k2 - 2 * (br - 2)
        where = lambda cond, a, b: lax.select(cond, jnp.int32(a), jnp.int32(b))
        k = jnp.int32(k)
        kk = jnp.maximum(jnp.int32(k), 0)
        k1 = jnp.maximum(jnp.int32(k1), 0)
        k2 = jnp.maximum(jnp.int32(k2), 0)
        k3 = jnp.maximum(jnp.int32(k3), 0)
        bi = where(k < inner, 1 + kk // (bc - 2), 0)
        bj = where(k < inner, 1 + kk % (bc - 2), 0)
        on1 = (k >= inner) & (k < inner + 2 * (bc - 2))
        bi = where(on1, (br - 1) * (k1 % 2), bi)
        bj = where(on1, 1 + k1 // 2, bj)
        on2 = (k >= inner + 2 * (bc - 2)) & (k < inner + 2 * (bc - 2) + 2 * (br - 2))
        bi = where(on2, 1 + k2 // 2, bi)
        bj = where(on2, (bc - 1) * (k2 % 2), bj)
        on3 = k >= inner + 2 * (bc - 2) + 2 * (br - 2)
        bi = where(on3, (br - 1) * (k3 // 2), bi)
        bj = where(on3, (bc - 1) * (k3 % 2), bj)
        return bi, bj

    def __call__(
        self, x_hbm, bias_ref, spread_ref, prec_ref, ch_ref, cv_ref, out_hbm, stein_ref,
        xp, sq, fo, klow0, klow1, st0, st1, cs0, cs1, qs0, qs1, wq, wv, whb, acc, ar_stage, ar1, ar2,
        load_sem, out_sem, hs_send, hs_recv, vs_send, vs_recv, a1_send, a1_recv, a2_send, a2_recv,
    ):
        rows, cols, n_gx, n_gy = self.rows, self.cols, self.n_gx, self.n_gy
        brows, bcols = self.brows, self.bcols
        gx, gy = lax.axis_index("gx"), lax.axis_index("gy")

        loads = [
            pltpu.make_async_copy(
                x_hbm.at[pl.ds(2 * i, 2)], xp.at[pl.ds(1 + 2 * i, 2), pl.ds(1, cols)], load_sem.at[i]
            )
            for i in range(brows)
        ]
        for copy in loads:
            copy.start()
        barrier = pltpu.get_barrier_semaphore()
        for off in range(1, n_gx):
            pl.semaphore_signal(
                barrier, inc=1, device_id={"gx": lax.rem(gx + off, n_gx), "gy": gy}, device_id_type=MESH
            )
        for off in range(1, n_gy):
            pl.semaphore_signal(
                barrier, inc=1, device_id={"gx": gx, "gy": lax.rem(gy + off, n_gy)}, device_id_type=MESH
            )

        minus_a = (-(prec_ref[...].astype(F32))).astype(BF16)
        h_mat, v_mat = ch_ref[...], cv_ref[...]
        h_t, v_t = h_mat.T, v_mat.T
        zero = jnp.zeros_like(h_mat)
        table = [
            [minus_a, h_mat, v_mat, zero],
            [h_t, minus_a, zero, v_mat],
            [v_t, zero, minus_a, h_mat],
            [zero, v_t, h_t, minus_a],
        ]
        for a in range(4):
            wq[64 * a : 64 * a + 64, :] = jnp.concatenate(table[a], axis=1)
        wv[0] = jnp.concatenate([zero, v_t], axis=1)
        wv[1] = jnp.concatenate([zero, v_mat], axis=1)
        for r in range(rows):
            parts = [p.astype(BF16) for p in split3(bias_ref[r])]
            tail = jnp.concatenate([jnp.zeros((16, 64), BF16)] + parts, axis=0)
            tail_t = tail.T
            whb[r, 0] = jnp.concatenate([h_t, tail_t], axis=1)
            whb[r, 1] = jnp.concatenate([h_mat, tail_t], axis=1)
        acc[...] = jnp.zeros_like(acc)

        def clear(row, row_count, col, col_count):
            def one(t, _):
                r, c = row + t // col_count, col + t % col_count
                xp[r, c] = jnp.zeros((64, 256), BF16)
                sq[r, c] = jnp.zeros((8, 256), F32)
                return 0

            lax.fori_loop(0, row_count * col_count, one, 0)

        has_up, has_down = gx > 0, gx < n_gx - 1
        has_left, has_right = gy > 0, gy < n_gy - 1
        pl.when(jnp.logical_not(has_up))(lambda: clear(0, 1, 1, cols))
        pl.when(jnp.logical_not(has_down))(lambda: clear(rows + 1, 1, 1, cols))
        pl.when(jnp.logical_not(has_left))(lambda: clear(1, rows, 0, 1))
        pl.when(jnp.logical_not(has_right))(lambda: clear(1, rows, cols + 1, 1))

        def down_copy(j):
            return pltpu.make_async_remote_copy(
                src_ref=x_hbm.at[pl.ds(rows - 1, 1), pl.ds(2 * j, 2)],
                dst_ref=xp.at[pl.ds(0, 1), pl.ds(1 + 2 * j, 2)],
                send_sem=vs_send.at[0, j], recv_sem=vs_recv.at[0, j],
                device_id={"gx": lax.rem(gx + 1, n_gx), "gy": gy}, device_id_type=MESH,
            )

        def up_copy(j):
            return pltpu.make_async_remote_copy(
                src_ref=x_hbm.at[pl.ds(0, 1), pl.ds(2 * j, 2)],
                dst_ref=xp.at[pl.ds(rows + 1, 1), pl.ds(1 + 2 * j, 2)],
                send_sem=vs_send.at[1, j], recv_sem=vs_recv.at[1, j],
                device_id={"gx": lax.rem(gx + n_gx - 1, n_gx), "gy": gy}, device_id_type=MESH,
            )

        def right_copy(i):
            return pltpu.make_async_remote_copy(
                src_ref=x_hbm.at[pl.ds(2 * i, 2), pl.ds(cols - 1, 1)],
                dst_ref=xp.at[pl.ds(1 + 2 * i, 2), pl.ds(0, 1)],
                send_sem=hs_send.at[0, i], recv_sem=hs_recv.at[0, i],
                device_id={"gx": gx, "gy": lax.rem(gy + 1, n_gy)}, device_id_type=MESH,
            )

        def left_copy(i):
            return pltpu.make_async_remote_copy(
                src_ref=x_hbm.at[pl.ds(2 * i, 2), pl.ds(0, 1)],
                dst_ref=xp.at[pl.ds(1 + 2 * i, 2), pl.ds(cols + 1, 1)],
                send_sem=hs_send.at[1, i], recv_sem=hs_recv.at[1, i],
                device_id={"gx": gx, "gy": lax.rem(gy + n_gy - 1, n_gy)}, device_id_type=MESH,
            )

        v_order = list(range(1, bcols - 1)) + [0, bcols - 1]
        h_order = list(range(1, brows - 1)) + [0, brows - 1]
        pl.semaphore_wait(barrier, n_gx + n_gy - 2)

        @pl.when(has_down)
        def _():
            for j in v_order:
                down_copy(j).start()

        @pl.when(has_up)
        def _():
            for j in v_order:
                up_copy(j).start()

        @pl.when(has_right)
        def _():
            for i in h_order:
                right_copy(i).start()

        @pl.when(has_left)
        def _():
            for i in h_order:
                left_copy(i).start()

        def norms(r, c):
            values = xp[r, c].astype(F32)
            sq[r, c] = replicated_sum(values * values)

        for i in range(brows):
            loads[i].wait()

            def norm_pair(t, _, i=i):
                norms(1 + 2 * i, 1 + t)
                norms(2 + 2 * i, 1 + t)
                return 0

            lax.fori_loop(0, cols, norm_pair, 0)

        def arrive(bi, bj):
            @pl.when((bi == 0) & has_up)
            def _():
                down_copy(bj).wait_recv()
                norms(0, 1 + 2 * bj)
                norms(0, 2 + 2 * bj)

            @pl.when((bi == brows - 1) & has_down)
            def _():
                up_copy(bj).wait_recv()
                norms(rows + 1, 1 + 2 * bj)
                norms(rows + 1, 2 + 2 * bj)

            @pl.when((bj == 0) & has_left)
            def _():
                right_copy(bi).wait_recv()
                norms(1 + 2 * bi, 0)
                norms(2 + 2 * bi, 0)

            @pl.when((bj == bcols - 1) & has_right)
            def _():
                left_copy(bi).wait_recv()
                norms(1 + 2 * bi, cols + 1)
                norms(2 + 2 * bi, cols + 1)

        row8 = lax.broadcasted_iota(jnp.int32, (8, 256), 0)
        hot_row = lax.broadcasted_iota(jnp.int32, (48, 256), 0)
        dims = (((1,), (0,)), ((), ()))
        dot = functools.partial(lax.dot_general, dimension_numbers=dims, preferred_element_type=F32)

        def stage_a(k, klow, st, cs, qs):
            bi, bj = self.block_of(k)
            r0, c0 = 1 + 2 * bi, 1 + 2 * bj
            at = lambda a, b: xp[r0 + a, c0 + b]
            own = [at(0, 0), at(0, 1), at(1, 0), at(1, 1)]
            q_rhs = jnp.concatenate(own, axis=0)
            q = dot(jnp.concatenate([q_rhs.T, wq[...]], axis=0), q_rhs)
            qs[...] = q
            for n in range(4):
                a, b = n // 2, n % 2
                va, hb = (-1, 2)[a], (-1, 2)[b]
                opposite, vert, horiz = own[3 - n], at(va, b), at(a, hb)
                total = (
                    (sq[r0 + a, c0 + b] + sq[r0 + va, c0 + b])
                    + (sq[r0 + a, c0 + hb] + sq[r0 + 1 - a, c0 + b])
                    + sq[r0 + a, c0 + 1 - b]
                )
                s1, s2, s3 = split3(total * -0.5)
                stack = lambda x0, x1: jnp.where(
                    row8 == x0, s1, jnp.where(row8 == x0 + 1, s2, jnp.where(row8 == x0 + 2, s3, jnp.where(
                        (row8 >= x1) & (row8 < x1 + 3), 1.0, 0.0)))
                )
                zeros8 = jnp.zeros((8, 256), F32)
                aug_r = jnp.concatenate([stack(3, 0), zeros8], axis=0).astype(BF16)
                aug_l = jnp.concatenate([stack(0, 3), zeros8], axis=0).astype(BF16)
                col = 2 * bj + b
                hot = jnp.where(
                    (hot_row == col) | (hot_row == col + 16) | (hot_row == col + 32), 1.0, 0.0
                ).astype(BF16)
                rhs = jnp.concatenate([opposite, vert, horiz, aug_r, hot], axis=0)
                lhs_t = jnp.concatenate([-opposite, vert, horiz, aug_l, jnp.zeros((48, 256), BF16)], axis=0)
                weight = jnp.concatenate([wv[a], whb[2 * bi + a, b]], axis=1)
                rest = dot(jnp.concatenate([lhs_t.T, weight], axis=0), rhs)
                h = spread_ref[2 * bi + a, 2 * bj + b]
                kernel = jnp.exp2((qs[0:256] + rest[0:256]) * (2.0 * LOG2E / h))
                klow[n] = kernel.astype(BF16)
                cs[n] = replicated_sum(kernel)
                score = qs[256 + 64 * n : 320 + 64 * n] + rest[256:320]
                st[n, 0:64] = score.astype(BF16)
                st[n, 64:128] = own[n]

        def stage_c(k, klow, st, cs):
            bi, bj = self.block_of(k)
            total = acc[...]
            for n in range(4):
                a, b = n // 2, n % 2
                h = spread_ref[2 * bi + a, 2 * bj + b]
                scale = 2.0 / h
                prod = dot(st[n], klow[n])
                pull, push = prod[0:64], prod[64:128]
                s = st[n, 0:64].astype(F32)
                x = st[n, 64:128].astype(F32)
                colsum = cs[n]
                v = (push - x * jnp.concatenate([colsum] * 8, axis=0)) * scale
                force = pull - v
                fo[2 * bi + a, 2 * bj + b] = force.astype(BF16)
                total = total + row_fold(s * (force - v)) + (2.0 * scale) * row_fold(x * v) + (8.0 * scale) * colsum
            acc[...] = total

        def out_copy(bi, bj):
            window = (pl.ds(2 * bi, 2), pl.ds(2 * bj, 2))
            return pltpu.make_async_copy(fo.at[window], out_hbm.at[window], out_sem.at[bi, bj])

        def ship(k):
            bi, bj = self.block_of(k)
            out_copy(bi, bj).start()

        blocks = brows * bcols
        set0, set1 = (klow0, st0, cs0), (klow1, st1, cs1)
        arrive(*self.block_of(0))
        stage_a(0, *set0, qs0)

        def body(j, _):
            arrive(*self.block_of(2 * j + 1))
            arrive(*self.block_of(2 * j + 2))
            stage_a(2 * j + 1, *set1, qs1)
            stage_c(2 * j, *set0)
            stage_a(2 * j + 2, *set0, qs0)
            stage_c(2 * j + 1, *set1)
            ship(2 * j)
            ship(2 * j + 1)
            return 0

        lax.fori_loop(0, blocks // 2 - 1, body, 0)
        arrive(*self.block_of(blocks - 1))
        stage_a(blocks - 1, *set1, qs1)
        stage_c(blocks - 2, *set0)
        stage_c(blocks - 1, *set1)
        ship(blocks - 2)
        ship(blocks - 1)

        ar_stage[0] = acc[:, 0:128] + acc[:, 128:256]
        ar1[gx] = ar_stage[0]

        def a1_copy(off):
            return pltpu.make_async_remote_copy(
                src_ref=ar_stage.at[0], dst_ref=ar1.at[gx],
                send_sem=a1_send.at[off - 1], recv_sem=a1_recv.at[off - 1],
                device_id={"gx": lax.rem(gx + off, n_gx), "gy": gy}, device_id_type=MESH,
            )

        def a2_copy(off):
            return pltpu.make_async_remote_copy(
                src_ref=ar_stage.at[1], dst_ref=ar2.at[gy],
                send_sem=a2_send.at[off - 1], recv_sem=a2_recv.at[off - 1],
                device_id={"gx": gx, "gy": lax.rem(gy + off, n_gy)}, device_id_type=MESH,
            )

        for off in range(1, n_gx):
            a1_copy(off).start()
        for off in range(1, n_gx):
            a1_copy(off).wait_recv()
        total = ar1[0]
        for i in range(1, n_gx):
            total = total + ar1[i]
        ar_stage[1] = total
        ar2[gy] = total
        for off in range(1, n_gy):
            a2_copy(off).start()
        for off in range(1, n_gy):
            a2_copy(off).wait_recv()
        total = ar2[0]
        for i in range(1, n_gy):
            total = total + ar2[i]
        pairs = float(rows * n_gx * cols * n_gy * 256 * 256)
        stein_ref[0, 0] = jnp.sum(total) / pairs

        for off in range(1, n_gx):
            a1_copy(off).wait_send()
        for off in range(1, n_gy):
            a2_copy(off).wait_send()

        @pl.when(has_down)
        def _():
            for j in v_order:
                down_copy(j).wait_send()

        @pl.when(has_up)
        def _():
            for j in v_order:
                up_copy(j).wait_send()

        @pl.when(has_right)
        def _():
            for i in h_order:
                right_copy(i).wait_send()

        @pl.when(has_left)
        def _():
            for i in h_order:
                left_copy(i).wait_send()

        for bi in range(brows):
            for bj in range(bcols):
                out_copy(bi, bj).wait()


def solution(mesh):
    n_gx, n_gy = mesh.shape["gx"], mesh.shape["gy"]

    def step(particles, bias, spread, precision, coupling_h, coupling_v):
        rows, cols = particles.shape[:2]
        dma = pltpu.SemaphoreType.DMA
        vmem = pl.BlockSpec(memory_space=pltpu.VMEM)
        hbm = pl.BlockSpec(memory_space=pl.ANY)
        smem = pl.BlockSpec(memory_space=pltpu.SMEM)
        force, stein = pl.pallas_call(
            Kernel(n_gx, n_gy, rows, cols),
            name="svgd",
            out_shape=(
                jax.ShapeDtypeStruct(particles.shape, BF16),
                jax.ShapeDtypeStruct((1, 1), F32),
            ),
            in_specs=[hbm, vmem, smem, vmem, vmem, vmem],
            out_specs=(hbm, smem),
            scratch_shapes=[
                pltpu.VMEM((rows + 2, cols + 2, 64, 256), BF16),
                pltpu.VMEM((rows + 2, cols + 2, 8, 256), F32),
                pltpu.VMEM((rows, cols, 64, 256), BF16),
                pltpu.VMEM((4, 256, 256), BF16),
                pltpu.VMEM((4, 256, 256), BF16),
                pltpu.VMEM((4, 128, 256), BF16),
                pltpu.VMEM((4, 128, 256), BF16),
                pltpu.VMEM((4, 8, 256), F32),
                pltpu.VMEM((4, 8, 256), F32),
                pltpu.VMEM((512, 256), F32),
                pltpu.VMEM((512, 256), F32),
                pltpu.VMEM((256, 256), BF16),
                pltpu.VMEM((2, 64, 128), BF16),
                pltpu.VMEM((rows, 2, 64, 128), BF16),
                pltpu.VMEM((8, 256), F32),
                pltpu.VMEM((2, 8, 128), F32),
                pltpu.VMEM((n_gx, 8, 128), F32),
                pltpu.VMEM((n_gy, 8, 128), F32),
                dma((rows // 2,)),
                dma((rows // 2, cols // 2)),
                dma((2, rows // 2)),
                dma((2, rows // 2)),
                dma((2, cols // 2)),
                dma((2, cols // 2)),
                dma((n_gx - 1,)),
                dma((n_gx - 1,)),
                dma((n_gy - 1,)),
                dma((n_gy - 1,)),
            ],
            compiler_params=pltpu.CompilerParams(collective_id=0, has_side_effects=True, vmem_limit_bytes=48 * 2**20),
        )(particles, bias, spread, precision, coupling_h, coupling_v)
        return force, stein[0, 0]

    return jax.shard_map(
        step,
        mesh=mesh,
        in_specs=(P("gx", "gy", None, None), P("gx", "gy", None), P("gx", "gy"), P(), P(), P()),
        out_specs=(P("gx", "gy", None, None), P()),
        check_vma=False,
    )
```

time: 285 us -> 47.8 us (0.17); the launches traced: 281 us -> 47.4 us
  other arithmetic: 77.8 us -> 0 us
  local copies, waits for them, and re-layouts: 82.2 us -> 5.69 us
  matrix products: 73.4 us -> 0 us
  Pallas kernels: 0 us -> 39.4 us
  blocking collectives: 33.9 us -> 0 us
  starting transfers between devices: 11.4 us -> 0 us
    slice x4 -> x0, local copies, waits for them, and re-layouts: 81.8 us -> none  [the longest x1 40.8 us: on_device(): own_dist[:, :-1]]
    reduce_sum x9 -> x0, other arithmetic: 77.8 us -> none  [the longest x1 60.5 us: on_device(): rowsum = jnp.sum(kernel, axis=-1)]
    dot_general x11 -> x0, matrix products: 73.4 us -> none  [the longest x2 21.3 us: mixing_t(): jnp.einsum('de,rcdp->rcep', matrix, states, preferred_element_type=jnp.fl...]
    pallas_call x0 -> x1, Pallas kernels: none -> 39.4 us  [step(): pl.pallas_call(Kernel(n_gx, n_gy, rows, cols), name='svgd', out_shape=(ja...]
    psum x4 -> x0, blocking collectives: 33.9 us -> none  [by_axis(): return functools.reduce(lax.psum, axes, x)]
    ppermute x4 -> x0, starting transfers between devices: 11.4 us -> none  [the longest x2 6.69 us: with_halo(): lax.ppermute(tail, axis, [(i, (i + 1) % count) for i in range(ends)])]
    unnamed x20 -> x11, local copies, waits for them, and re-layouts: 0.39 us -> 5.69 us
  transfers between devices with their start and end apart: 4 -> 0, of which waited for: 0 -> 0; matrix products, arithmetic and copies ran while one was open for 40% -> 0% of each run, Pallas kernels for 0% -> 0%
where the time goes in v1:
time: 47.8 us; the launch traced here: 47.4 us
  Pallas kernels  39.4 us (82%)
  local copies, waits for them, and re-layouts  5.69 us (12%)
  between operations  2.34 us (5%)
    pallas_call x1, Pallas kernels, step(): pl.pallas_call(Kernel(n_gx, n_gy, rows, cols), name='svgd', out_shape=(ja...  39.4 us
    unnamed x11, local copies, waits for them, and re-layouts  5.69 us

profile of v1, /device:TPU:1, one launch (start us, length us, event | category | flops | bytes accessed | tf_op | source)
XLA Modules:
  0.0 47.4 jit_solution(5670354231176905148)
XLA Ops:
  0.6 0.0 copy-start
  0.6 0.8 %copy-done = f32[8,16,64]{2,1,0:T(8,128)S(1)} copy-done((f32[8,16,64]{2,1,0:T(8,128)S(1)}, f32[8,16,64]{2,1,0:T(8,128)}, u32[]{:S(2)}) %copy-start) | copy-done | bytes 32792
  1.5 0.0 copy-start.1
  1.5 0.7 %copy-done.1 = bf16[64,64]{1,0:T(8,128)(2,1)S(1)} copy-done((bf16[64,64]{1,0:T(8,128)(2,1)S(1)}, bf16[64,64]{1,0:T(8,128)(2,1)}, u32[]{:S(2)}) %copy-start.1) | copy-done | bytes 8216
  2.2 0.0 copy-start.2
  2.2 0.7 %copy-done.2 = bf16[64,64]{1,0:T(8,128)(2,1)S(1)} copy-done((bf16[64,64]{1,0:T(8,128)(2,1)S(1)}, bf16[64,64]{1,0:T(8,128)(2,1)}, u32[]{:S(2)}) %copy-start.2) | copy-done | bytes 8216
  2.9 0.0 copy-start.3
  2.9 0.7 %copy-done.3 = bf16[64,64]{1,0:T(8,128)(2,1)S(1)} copy-done((bf16[64,64]{1,0:T(8,128)(2,1)S(1)}, bf16[64,64]{1,0:T(8,128)(2,1)}, u32[]{:S(2)}) %copy-start.3) | copy-done | bytes 8216
  3.6 0.0 copy-start.4
  3.6 0.7 %copy-done.4 = f32[8,16]{1,0:T(8,128)S(1)} copy-done((f32[8,16]{1,0:T(8,128)S(1)}, f32[8,16]{1,0:T(8,128)}, u32[]{:S(2)}) %copy-start.4) | copy-done | bytes 536
  4.3 39.4 %svgd.1 = (bf16[8,16,64,256]{3,2,1,0:T(8,128)(2,1)S(1)}, f32[1,1]{1,0:T(1,128)}) custom-call(bf16[8,16,64,256]{3,2,1,0:T(8,128)(2,1)} %x_hbm.1, f32[8,16,64]{2,1,0:T(8,128)S(1)} %copy-done, f32[8,16]{1,0:T(8,128)S(1)} %copy-done.4, bf16[64,64]{1,0:T(8,128)(2,1)S(1)} %copy-done.1, bf16[64,64]{1,0:T(8,128)(2,1)S(1)} %copy-done.2, bf16[64,64]{1,0:T(8,128)(2,1)S(1)} %copy-done.3), custom_call_target="tpu_custom_call" | custom-call | tf_op jit(solution)/shard_map/svgd/pallas_call | solution.py:402
  43.7 2.0 %copy.10 = bf16[8,16,64,256]{3,2,1,0:T(8,128)(2,1)} copy(bf16[8,16,64,256]{3,2,1,0:T(8,128)(2,1)S(1)} %get-tuple-element.8) | data formatting | bytes 8388608
Async XLA Ops:
  0.6 0.8 %copy-start = (f32[8,16,64]{2,1,0:T(8,128)S(1)}, f32[8,16,64]{2,1,0:T(8,128)}, u32[]{:S(2)}) copy-start(f32[8,16,64]{2,1,0:T(8,128)} %bias_ref.1) | copy-start | bytes 98308
  1.5 0.7 %copy-start.1 = (bf16[64,64]{1,0:T(8,128)(2,1)S(1)}, bf16[64,64]{1,0:T(8,128)(2,1)}, u32[]{:S(2)}) copy-start(bf16[64,64]{1,0:T(8,128)(2,1)} %prec_ref.1) | copy-start | bytes 24580
  2.2 0.7 %copy-start.2 = (bf16[64,64]{1,0:T(8,128)(2,1)S(1)}, bf16[64,64]{1,0:T(8,128)(2,1)}, u32[]{:S(2)}) copy-start(bf16[64,64]{1,0:T(8,128)(2,1)} %ch_ref.1) | copy-start | bytes 24580
  2.9 0.7 %copy-start.3 = (bf16[64,64]{1,0:T(8,128)(2,1)S(1)}, bf16[64,64]{1,0:T(8,128)(2,1)}, u32[]{:S(2)}) copy-start(bf16[64,64]{1,0:T(8,128)(2,1)} %cv_ref.1) | copy-start | bytes 24580
  3.6 0.7 %copy-start.4 = (f32[8,16]{1,0:T(8,128)S(1)}, f32[8,16]{1,0:T(8,128)}, u32[]{:S(2)}) copy-start(f32[8,16]{1,0:T(8,128)} %spread_ref.1) | copy-start | bytes 1540

commit v2 on v1

--- a/solution.py
+++ b/solution.py
@@ -69,8 +69,8 @@
         return bi, bj
 
     def __call__(
-        self, x_hbm, bias_ref, spread_ref, prec_ref, ch_ref, cv_ref, out_hbm, stein_ref,
-        xp, sq, fo, klow0, klow1, st0, st1, cs0, cs1, qs0, qs1, wq, wv, whb, acc, ar_stage, ar1, ar2,
+        self, x_hbm, bias_hbm, spread_hbm, prec_hbm, ch_hbm, cv_hbm, out_hbm, stein_ref,
+        bias_ref, spread_ref, prec_ref, ch_ref, cv_ref, small_sem, xp, sq, fo, klow, st, qs, hot, base_l, base_r, wq, wv, whb, acc, ar_stage, ar1, ar2,
         load_sem, out_sem, hs_send, hs_recv, vs_send, vs_recv, a1_send, a1_recv, a2_send, a2_recv,
     ):
         rows, cols, n_gx, n_gy = self.rows, self.cols, self.n_gx, self.n_gy
@@ -83,7 +83,13 @@
             )
             for i in range(brows)
         ]
-        for copy in loads:
+        smalls = [
+            pltpu.make_async_copy(src, dst, small_sem.at[i])
+            for i, (src, dst) in enumerate(
+                [(prec_hbm, prec_ref), (ch_hbm, ch_ref), (cv_hbm, cv_ref), (bias_hbm, bias_ref), (spread_hbm, spread_ref)]
+            )
+        ]
+        for copy in smalls + loads:
             copy.start()
         barrier = pltpu.get_barrier_semaphore()
         for off in range(1, n_gx):
@@ -95,6 +101,8 @@
                 barrier, inc=1, device_id={"gx": gx, "gy": lax.rem(gy + off, n_gy)}, device_id_type=MESH
             )
 
+        for copy in smalls:
+            copy.wait()
         minus_a = (-(prec_ref[...].astype(F32))).astype(BF16)
         h_mat, v_mat = ch_ref[...], cv_ref[...]
         h_t, v_t = h_mat.T, v_mat.T
@@ -116,6 +124,19 @@
             whb[r, 0] = jnp.concatenate([h_t, tail_t], axis=1)
             whb[r, 1] = jnp.concatenate([h_mat, tail_t], axis=1)
         acc[...] = jnp.zeros_like(acc)
+        row = lax.broadcasted_iota(jnp.int32, (8, 256), 0)
+        for slot in range(2):
+            for n in range(4):
+                st[slot, n, 128:144] = jnp.ones((16, 256), BF16)
+        base_r[...] = jnp.where(row < 3, 1.0, 0.0)
+        base_l[...] = jnp.where((row >= 3) & (row < 6), 1.0, 0.0)
+        hot_row = lax.broadcasted_iota(jnp.int32, (48, 256), 0) % 16
+
+        def one_hot(col, _):
+            hot[col] = jnp.where(hot_row == col, 1.0, 0.0).astype(BF16)
+            return 0
+
+        lax.fori_loop(0, cols, one_hot, 0)
 
         def clear(row, row_count, col, col_count):
             def one(t, _):
@@ -229,18 +250,16 @@
                 norms(2 + 2 * bi, cols + 1)
 
         row8 = lax.broadcasted_iota(jnp.int32, (8, 256), 0)
-        hot_row = lax.broadcasted_iota(jnp.int32, (48, 256), 0)
         dims = (((1,), (0,)), ((), ()))
         dot = functools.partial(lax.dot_general, dimension_numbers=dims, preferred_element_type=F32)
 
-        def stage_a(k, klow, st, cs, qs):
+        def stage_a(k, slot):
             bi, bj = self.block_of(k)
             r0, c0 = 1 + 2 * bi, 1 + 2 * bj
             at = lambda a, b: xp[r0 + a, c0 + b]
             own = [at(0, 0), at(0, 1), at(1, 0), at(1, 1)]
             q_rhs = jnp.concatenate(own, axis=0)
-            q = dot(jnp.concatenate([q_rhs.T, wq[...]], axis=0), q_rhs)
-            qs[...] = q
+            qs[slot] = dot(jnp.concatenate([q_rhs.T, wq[...]], axis=0), q_rhs)
             for n in range(4):
                 a, b = n // 2, n % 2
                 va, hb = (-1, 2)[a], (-1, 2)[b]
@@ -251,41 +270,34 @@
                     + sq[r0 + a, c0 + 1 - b]
                 )
                 s1, s2, s3 = split3(total * -0.5)
-                stack = lambda x0, x1: jnp.where(
-                    row8 == x0, s1, jnp.where(row8 == x0 + 1, s2, jnp.where(row8 == x0 + 2, s3, jnp.where(
-                        (row8 >= x1) & (row8 < x1 + 3), 1.0, 0.0)))
+                pick = lambda base, x: jnp.where(
+                    row8 == x, s1, jnp.where(row8 == x + 1, s2, jnp.where(row8 == x + 2, s3, base[...]))
                 )
                 zeros8 = jnp.zeros((8, 256), F32)
-                aug_r = jnp.concatenate([stack(3, 0), zeros8], axis=0).astype(BF16)
-                aug_l = jnp.concatenate([stack(0, 3), zeros8], axis=0).astype(BF16)
-                col = 2 * bj + b
-                hot = jnp.where(
-                    (hot_row == col) | (hot_row == col + 16) | (hot_row == col + 32), 1.0, 0.0
-                ).astype(BF16)
-                rhs = jnp.concatenate([opposite, vert, horiz, aug_r, hot], axis=0)
+                aug_r = jnp.concatenate([pick(base_r, 3), zeros8], axis=0).astype(BF16)
+                aug_l = jnp.concatenate([pick(base_l, 0), zeros8], axis=0).astype(BF16)
+                rhs = jnp.concatenate([opposite, vert, horiz, aug_r, hot[2 * bj + b]], axis=0)
                 lhs_t = jnp.concatenate([-opposite, vert, horiz, aug_l, jnp.zeros((48, 256), BF16)], axis=0)
                 weight = jnp.concatenate([wv[a], whb[2 * bi + a, b]], axis=1)
                 rest = dot(jnp.concatenate([lhs_t.T, weight], axis=0), rhs)
                 h = spread_ref[2 * bi + a, 2 * bj + b]
-                kernel = jnp.exp2((qs[0:256] + rest[0:256]) * (2.0 * LOG2E / h))
-                klow[n] = kernel.astype(BF16)
-                cs[n] = replicated_sum(kernel)
-                score = qs[256 + 64 * n : 320 + 64 * n] + rest[256:320]
-                st[n, 0:64] = score.astype(BF16)
-                st[n, 64:128] = own[n]
-
-        def stage_c(k, klow, st, cs):
+                kernel = jnp.exp2((qs[slot, 0:256] + rest[0:256]) * (2.0 * LOG2E / h))
+                klow[slot, n] = kernel.astype(BF16)
+                score = qs[slot, 256 + 64 * n : 320 + 64 * n] + rest[256:320]
+                st[slot, n, 0:64] = score.astype(BF16)
+                st[slot, n, 64:128] = own[n]
+
+        def stage_c(k, slot):
             bi, bj = self.block_of(k)
             total = acc[...]
             for n in range(4):
                 a, b = n // 2, n % 2
                 h = spread_ref[2 * bi + a, 2 * bj + b]
                 scale = 2.0 / h
-                prod = dot(st[n], klow[n])
-                pull, push = prod[0:64], prod[64:128]
-                s = st[n, 0:64].astype(F32)
-                x = st[n, 64:128].astype(F32)
-                colsum = cs[n]
+                prod = dot(st[slot, n], klow[slot, n])
+                pull, push, colsum = prod[0:64], prod[64:128], prod[128:136]
+                s = st[slot, n, 0:64].astype(F32)
+                x = st[slot, n, 64:128].astype(F32)
                 v = (push - x * jnp.concatenate([colsum] * 8, axis=0)) * scale
                 force = pull - v
                 fo[2 * bi + a, 2 * bj + b] = force.astype(BF16)
@@ -301,26 +313,29 @@
             out_copy(bi, bj).start()
 
         blocks = brows * bcols
-        set0, set1 = (klow0, st0, cs0), (klow1, st1, cs1)
-        arrive(*self.block_of(0))
-        stage_a(0, *set0, qs0)
+
+        def pair_arrives(j):
+            @pl.when(2 * j + 1 >= (brows - 2) * (bcols - 2))
+            def _():
+                arrive(*self.block_of(2 * j))
+                arrive(*self.block_of(2 * j + 1))
+
+        stage_a(0, 0)
+        stage_a(1, 1)
 
         def body(j, _):
-            arrive(*self.block_of(2 * j + 1))
-            arrive(*self.block_of(2 * j + 2))
-            stage_a(2 * j + 1, *set1, qs1)
-            stage_c(2 * j, *set0)
-            stage_a(2 * j + 2, *set0, qs0)
-            stage_c(2 * j + 1, *set1)
+            pair_arrives(j + 1)
+            stage_c(2 * j, 0)
+            stage_c(2 * j + 1, 1)
+            stage_a(2 * j + 2, 0)
+            stage_a(2 * j + 3, 1)
             ship(2 * j)
             ship(2 * j + 1)
             return 0
 
         lax.fori_loop(0, blocks // 2 - 1, body, 0)
-        arrive(*self.block_of(blocks - 1))
-        stage_a(blocks - 1, *set1, qs1)
-        stage_c(blocks - 2, *set0)
-        stage_c(blocks - 1, *set1)
+        stage_c(blocks - 2, 0)
+        stage_c(blocks - 1, 1)
         ship(blocks - 2)
         ship(blocks - 1)
 
@@ -396,8 +411,7 @@
     def step(particles, bias, spread, precision, coupling_h, coupling_v):
         rows, cols = particles.shape[:2]
         dma = pltpu.SemaphoreType.DMA
-        vmem = pl.BlockSpec(memory_space=pltpu.VMEM)
-        hbm = pl.BlockSpec(memory_space=pl.ANY)
+        hbm = pl.BlockSpec(memory_space=pltpu.HBM)
         smem = pl.BlockSpec(memory_space=pltpu.SMEM)
         force, stein = pl.pallas_call(
             Kernel(n_gx, n_gy, rows, cols),
@@ -406,20 +420,24 @@
                 jax.ShapeDtypeStruct(particles.shape, BF16),
                 jax.ShapeDtypeStruct((1, 1), F32),
             ),
-            in_specs=[hbm, vmem, smem, vmem, vmem, vmem],
+            in_specs=[hbm] * 6,
             out_specs=(hbm, smem),
             scratch_shapes=[
+                pltpu.VMEM(bias.shape, F32),
+                pltpu.SMEM(spread.shape, F32),
+                pltpu.VMEM((64, 64), BF16),
+                pltpu.VMEM((64, 64), BF16),
+                pltpu.VMEM((64, 64), BF16),
+                dma((5,)),
                 pltpu.VMEM((rows + 2, cols + 2, 64, 256), BF16),
                 pltpu.VMEM((rows + 2, cols + 2, 8, 256), F32),
                 pltpu.VMEM((rows, cols, 64, 256), BF16),
-                pltpu.VMEM((4, 256, 256), BF16),
-                pltpu.VMEM((4, 256, 256), BF16),
-                pltpu.VMEM((4, 128, 256), BF16),
-                pltpu.VMEM((4, 128, 256), BF16),
-                pltpu.VMEM((4, 8, 256), F32),
-                pltpu.VMEM((4, 8, 256), F32),
-                pltpu.VMEM((512, 256), F32),
-                pltpu.VMEM((512, 256), F32),
+                pltpu.VMEM((2, 4, 256, 256), BF16),
+                pltpu.VMEM((2, 4, 144, 256), BF16),
+                pltpu.VMEM((2, 512, 256), F32),
+                pltpu.VMEM((cols, 48, 256), BF16),
+                pltpu.VMEM((8, 256), F32),
+                pltpu.VMEM((8, 256), F32),
                 pltpu.VMEM((256, 256), BF16),
                 pltpu.VMEM((2, 64, 128), BF16),
                 pltpu.VMEM((rows, 2, 64, 128), BF16),
@@ -438,8 +456,8 @@
                 dma((n_gy - 1,)),
                 dma((n_gy - 1,)),
             ],
-            compiler_params=pltpu.CompilerParams(collective_id=0, has_side_effects=True, vmem_limit_bytes=48 * 2**20),
-        )(particles, bias, spread, precision, coupling_h, coupling_v)
+            compiler_params=pltpu.CompilerParams(collective_id=0, has_side_effects=True, vmem_limit_bytes=50_000_000),
+        )(particles, *(pltpu.with_memory_space_constraint(v, pltpu.HBM) for v in (bias, spread, precision, coupling_h, coupling_v)))
         return force, stein[0, 0]
 
     return jax.shard_map(

time: 47.8 us -> 43.3 us (0.906)
  local copies, waits for them, and re-layouts: 5.69 us -> 2.02 us
  Pallas kernels: 39.4 us -> 38.8 us
    unnamed x11 -> x1, local copies, waits for them, and re-layouts: 5.69 us -> 2.02 us
    pallas_call x1, Pallas kernels: 39.4 us -> 38.8 us  [step(): pl.pallas_call(Kernel(n_gx, n_gy, rows, cols), name='svgd', out_shape=(ja...]
where the time goes in v2:
time: 43.3 us; the launch traced here: 43.1 us
  Pallas kernels  38.8 us (90%)
  between operations  2.33 us (5%)
  local copies, waits for them, and re-layouts  2.02 us (5%)
    pallas_call x1, Pallas kernels, step(): pl.pallas_call(Kernel(n_gx, n_gy, rows, cols), name='svgd', out_shape=(ja...  38.8 us
    unnamed x1, local copies, waits for them, and re-layouts  2.02 us

profile of v2, /device:TPU:1, one launch (start us, length us, event | category | flops | bytes accessed | tf_op | source)
XLA Modules:
  0.0 43.1 jit_solution(9580752674330767156)
XLA Ops:
  0.6 38.8 %svgd.1 = (bf16[8,16,64,256]{3,2,1,0:T(8,128)(2,1)S(1)}, f32[1,1]{1,0:T(1,128)}) custom-call(bf16[8,16,64,256]{3,2,1,0:T(8,128)(2,1)} %x_hbm.1, f32[8,16,64]{2,1,0:T(8,128)} %bias_hbm.1, f32[8,16]{1,0:T(8,128)} %spread_hbm.1, bf16[64,64]{1,0:T(8,128)(2,1)} %prec_hbm.1, bf16[64,64]{1,0:T(8,128)(2,1)} %ch_hbm.1, bf16[64,64]{1,0:T(8,128)(2,1)} %cv_hbm.1), custom_call_target="tpu_custom_call" | custom-call | tf_op jit(solution)/shard_map/svgd/pallas_call | solution.py:416
  39.4 2.0 %copy.10 = bf16[8,16,64,256]{3,2,1,0:T(8,128)(2,1)} copy(bf16[8,16,64,256]{3,2,1,0:T(8,128)(2,1)S(1)} %get-tuple-element.8) | data formatting | bytes 8388608

commit v3 on v2

--- a/solution.py
+++ b/solution.py
@@ -69,9 +69,9 @@
         return bi, bj
 
     def __call__(
-        self, x_hbm, bias_hbm, spread_hbm, prec_hbm, ch_hbm, cv_hbm, out_hbm, stein_ref,
-        bias_ref, spread_ref, prec_ref, ch_ref, cv_ref, small_sem, xp, sq, fo, klow, st, qs, hot, base_l, base_r, wq, wv, whb, acc, ar_stage, ar1, ar2,
-        load_sem, out_sem, hs_send, hs_recv, vs_send, vs_recv, a1_send, a1_recv, a2_send, a2_recv,
+        self, x_hbm, bias_hbm, spread_hbm, prec_hbm, ch_hbm, cv_hbm, fo, stein_ref,
+        bias_ref, spread_ref, prec_ref, ch_ref, cv_ref, small_sem, xp, sq, klow, st, qs, hot, base_l, base_r, wq, wv, whb, acc, ar_stage, ar_all,
+        load_sem, hs_send, hs_recv, vs_send, vs_recv, ar_send, ar_recv, ready,
     ):
         rows, cols, n_gx, n_gy = self.rows, self.cols, self.n_gx, self.n_gy
         brows, bcols = self.brows, self.bcols
@@ -188,28 +188,6 @@
 
         v_order = list(range(1, bcols - 1)) + [0, bcols - 1]
         h_order = list(range(1, brows - 1)) + [0, brows - 1]
-        pl.semaphore_wait(barrier, n_gx + n_gy - 2)
-
-        @pl.when(has_down)
-        def _():
-            for j in v_order:
-                down_copy(j).start()
-
-        @pl.when(has_up)
-        def _():
-            for j in v_order:
-                up_copy(j).start()
-
-        @pl.when(has_right)
-        def _():
-            for i in h_order:
-                right_copy(i).start()
-
-        @pl.when(has_left)
-        def _():
-            for i in h_order:
-                left_copy(i).start()
-
         def norms(r, c):
             values = xp[r, c].astype(F32)
             sq[r, c] = replicated_sum(values * values)
@@ -260,7 +238,8 @@
             own = [at(0, 0), at(0, 1), at(1, 0), at(1, 1)]
             q_rhs = jnp.concatenate(own, axis=0)
             qs[slot] = dot(jnp.concatenate([q_rhs.T, wq[...]], axis=0), q_rhs)
-            for n in range(4):
+
+            def node(n):
                 a, b = n // 2, n % 2
                 va, hb = (-1, 2)[a], (-1, 2)[b]
                 opposite, vert, horiz = own[3 - n], at(va, b), at(a, hb)
@@ -287,10 +266,12 @@
                 st[slot, n, 0:64] = score.astype(BF16)
                 st[slot, n, 64:128] = own[n]
 
+            return node
+
         def stage_c(k, slot):
             bi, bj = self.block_of(k)
-            total = acc[...]
-            for n in range(4):
+
+            def node(n):
                 a, b = n // 2, n % 2
                 h = spread_ref[2 * bi + a, 2 * bj + b]
                 scale = 2.0 / h
@@ -301,84 +282,105 @@
                 v = (push - x * jnp.concatenate([colsum] * 8, axis=0)) * scale
                 force = pull - v
                 fo[2 * bi + a, 2 * bj + b] = force.astype(BF16)
-                total = total + row_fold(s * (force - v)) + (2.0 * scale) * row_fold(x * v) + (8.0 * scale) * colsum
-            acc[...] = total
-
-        def out_copy(bi, bj):
-            window = (pl.ds(2 * bi, 2), pl.ds(2 * bj, 2))
-            return pltpu.make_async_copy(fo.at[window], out_hbm.at[window], out_sem.at[bi, bj])
-
-        def ship(k):
-            bi, bj = self.block_of(k)
-            out_copy(bi, bj).start()
+                acc[...] += row_fold(s * (force - v)) + (2.0 * scale) * row_fold(x * v) + (8.0 * scale) * colsum
+
+            return node
 
         blocks = brows * bcols
 
         def pair_arrives(j):
             @pl.when(2 * j + 1 >= (brows - 2) * (bcols - 2))
             def _():
-                arrive(*self.block_of(2 * j))
-                arrive(*self.block_of(2 * j + 1))
-
-        stage_a(0, 0)
-        stage_a(1, 1)
+                def one(u, _):
+                    arrive(*self.block_of(2 * j + u))
+                    return 0
+
+                lax.fori_loop(0, 2, one, 0)
+
+        for slot in range(2):
+            node = stage_a(slot, slot)
+            for n in range(4):
+                node(n)
+
+        pl.semaphore_wait(barrier, n_gx + n_gy - 2)
+        for off in range(1, n_gx):
+            pl.semaphore_signal(
+                ready, inc=1, device_id={"gx": lax.rem(gx + off, n_gx), "gy": gy}, device_id_type=MESH
+            )
+
+        @pl.when(has_down)
+        def _():
+            for j in v_order:
+                down_copy(j).start()
+
+        @pl.when(has_up)
+        def _():
+            for j in v_order:
+                up_copy(j).start()
+
+        @pl.when(has_right)
+        def _():
+            for i in h_order:
+                right_copy(i).start()
+
+        @pl.when(has_left)
+        def _():
+            for i in h_order:
+                left_copy(i).start()
+
+        unroll = 3
 
         def body(j, _):
-            pair_arrives(j + 1)
-            stage_c(2 * j, 0)
-            stage_c(2 * j + 1, 1)
-            stage_a(2 * j + 2, 0)
-            stage_a(2 * j + 3, 1)
-            ship(2 * j)
-            ship(2 * j + 1)
+            for u in range(unroll):
+                pair_arrives(unroll * j + u + 1)
+            for u in range(unroll):
+                p = unroll * j + u
+                for slot in range(2):
+                    behind, ahead = stage_c(2 * p + slot, slot), stage_a(2 * p + 2 + slot, slot)
+                    for n in range(4):
+                        behind(n)
+                        ahead(n)
             return 0
 
-        lax.fori_loop(0, blocks // 2 - 1, body, 0)
-        stage_c(blocks - 2, 0)
-        stage_c(blocks - 1, 1)
-        ship(blocks - 2)
-        ship(blocks - 1)
-
-        ar_stage[0] = acc[:, 0:128] + acc[:, 128:256]
-        ar1[gx] = ar_stage[0]
-
-        def a1_copy(off):
+        lax.fori_loop(0, (blocks // 2 - 1) // unroll, body, 0)
+        for slot in range(2):
+            node = stage_c(blocks - 2 + slot, slot)
+            for n in range(4):
+                node(n)
+
+        mine = jnp.sum(acc[:, 0:128] + acc[:, 128:256], axis=0, keepdims=True)
+        me = gx * n_gy + gy
+        ar_stage[0] = mine
+        ar_all[me] = mine
+
+        def ring(d, n):
+            return min(d % n, n - d % n)
+
+        def distance(off):
+            z = (ring(off[0] // 2, n_gx // 2) + ring((off[0] + 1) // 2, n_gx // 2)) / 2
+            y = (ring(off[1] // 4, 4) * (4 - off[1] % 4) + ring(off[1] // 4 + 1, 4) * (off[1] % 4)) / 4
+            return z + y + ring(off[1], 4)
+
+        offs = [(i, j) for i in range(n_gx) for j in range(n_gy) if i or j]
+        offs.sort(key=distance, reverse=True)
+
+        def sum_copy(t):
+            i, j = offs[t]
             return pltpu.make_async_remote_copy(
-                src_ref=ar_stage.at[0], dst_ref=ar1.at[gx],
-                send_sem=a1_send.at[off - 1], recv_sem=a1_recv.at[off - 1],
-                device_id={"gx": lax.rem(gx + off, n_gx), "gy": gy}, device_id_type=MESH,
-            )
-
-        def a2_copy(off):
-            return pltpu.make_async_remote_copy(
-                src_ref=ar_stage.at[1], dst_ref=ar2.at[gy],
-                send_sem=a2_send.at[off - 1], recv_sem=a2_recv.at[off - 1],
-                device_id={"gx": gx, "gy": lax.rem(gy + off, n_gy)}, device_id_type=MESH,
-            )
-
-        for off in range(1, n_gx):
-            a1_copy(off).start()
-        for off in range(1, n_gx):
-            a1_copy(off).wait_recv()
-        total = ar1[0]
-        for i in range(1, n_gx):
-            total = total + ar1[i]
-        ar_stage[1] = total
-        ar2[gy] = total
-        for off in range(1, n_gy):
-            a2_copy(off).start()
-        for off in range(1, n_gy):
-            a2_copy(off).wait_recv()
-        total = ar2[0]
-        for i in range(1, n_gy):
-            total = total + ar2[i]
+                src_ref=ar_stage, dst_ref=ar_all.at[pl.ds(me, 1)], send_sem=ar_send.at[t], recv_sem=ar_recv.at[t],
+                device_id={"gx": lax.rem(gx + i, n_gx), "gy": lax.rem(gy + j, n_gy)}, device_id_type=MESH,
+            )
+
+        pl.semaphore_wait(ready, n_gx - 1)
+        for t in range(len(offs)):
+            sum_copy(t).start()
+        for t in range(len(offs)):
+            sum_copy(t).wait_recv()
         pairs = float(rows * n_gx * cols * n_gy * 256 * 256)
-        stein_ref[0, 0] = jnp.sum(total) / pairs
-
-        for off in range(1, n_gx):
-            a1_copy(off).wait_send()
-        for off in range(1, n_gy):
-            a2_copy(off).wait_send()
+        stein_ref[0, 0] = jnp.sum(ar_all[...]) / pairs
+
+        for t in range(len(offs)):
+            sum_copy(t).wait_send()
 
         @pl.when(has_down)
         def _():
@@ -399,10 +401,6 @@
         def _():
             for i in h_order:
                 left_copy(i).wait_send()
-
-        for bi in range(brows):
-            for bj in range(bcols):
-                out_copy(bi, bj).wait()
 
 
 def solution(mesh):
@@ -421,7 +419,7 @@
                 jax.ShapeDtypeStruct((1, 1), F32),
             ),
             in_specs=[hbm] * 6,
-            out_specs=(hbm, smem),
+            out_specs=(pl.BlockSpec(memory_space=pltpu.VMEM), smem),
             scratch_shapes=[
                 pltpu.VMEM(bias.shape, F32),
                 pltpu.SMEM(spread.shape, F32),
@@ -431,7 +429,6 @@
                 dma((5,)),
                 pltpu.VMEM((rows + 2, cols + 2, 64, 256), BF16),
                 pltpu.VMEM((rows + 2, cols + 2, 8, 256), F32),
-                pltpu.VMEM((rows, cols, 64, 256), BF16),
                 pltpu.VMEM((2, 4, 256, 256), BF16),
                 pltpu.VMEM((2, 4, 144, 256), BF16),
                 pltpu.VMEM((2, 512, 256), F32),
@@ -442,19 +439,16 @@
                 pltpu.VMEM((2, 64, 128), BF16),
                 pltpu.VMEM((rows, 2, 64, 128), BF16),
                 pltpu.VMEM((8, 256), F32),
-                pltpu.VMEM((2, 8, 128), F32),
-                pltpu.VMEM((n_gx, 8, 128), F32),
-                pltpu.VMEM((n_gy, 8, 128), F32),
+                pltpu.VMEM((1, 1, 128), F32),
+                pltpu.VMEM((n_gx * n_gy, 1, 128), F32),
                 dma((rows // 2,)),
-                dma((rows // 2, cols // 2)),
                 dma((2, rows // 2)),
                 dma((2, rows // 2)),
                 dma((2, cols // 2)),
                 dma((2, cols // 2)),
-                dma((n_gx - 1,)),
-                dma((n_gx - 1,)),
-                dma((n_gy - 1,)),
-                dma((n_gy - 1,)),
+                dma((n_gx * n_gy - 1,)),
+                dma((n_gx * n_gy - 1,)),
+                pltpu.SemaphoreType.REGULAR,
             ],
             compiler_params=pltpu.CompilerParams(collective_id=0, has_side_effects=True, vmem_limit_bytes=50_000_000),
         )(particles, *(pltpu.with_memory_space_constraint(v, pltpu.HBM) for v in (bias, spread, precision, coupling_h, coupling_v)))

time: 43.3 us -> 39.2 us (0.905)
  Pallas kernels: 38.8 us -> 34.7 us
    pallas_call x1, Pallas kernels: 38.8 us -> 34.7 us  [step(): pl.pallas_call(Kernel(n_gx, n_gy, rows, cols), name='svgd', out_shape=(ja...]
where the time goes in v3:
time: 39.2 us; the launch traced here: 39 us
  Pallas kernels  34.7 us (89%)
  between operations  2.33 us (6%)
  local copies, waits for them, and re-layouts  2.02 us (5%)
    pallas_call x1, Pallas kernels, step(): pl.pallas_call(Kernel(n_gx, n_gy, rows, cols), name='svgd', out_shape=(ja...  34.7 us
    unnamed x1, local copies, waits for them, and re-layouts  2.02 us

profile of v3, /device:TPU:1, one launch (start us, length us, event | category | flops | bytes accessed | tf_op | source)
XLA Modules:
  0.0 39.0 jit_solution(2487929374808089272)
XLA Ops:
  0.6 34.7 %svgd.1 = (bf16[8,16,64,256]{3,2,1,0:T(8,128)(2,1)S(1)}, f32[1,1]{1,0:T(1,128)}) custom-call(bf16[8,16,64,256]{3,2,1,0:T(8,128)(2,1)} %x_hbm.1, f32[8,16,64]{2,1,0:T(8,128)} %bias_hbm.1, f32[8,16]{1,0:T(8,128)} %spread_hbm.1, bf16[64,64]{1,0:T(8,128)(2,1)} %prec_hbm.1, bf16[64,64]{1,0:T(8,128)(2,1)} %ch_hbm.1, bf16[64,64]{1,0:T(8,128)(2,1)} %cv_hbm.1), custom_call_target="tpu_custom_call" | custom-call | tf_op jit(solution)/shard_map/svgd/pallas_call | solution.py:414
  35.3 2.0 %copy.10 = bf16[8,16,64,256]{3,2,1,0:T(8,128)(2,1)} copy(bf16[8,16,64,256]{3,2,1,0:T(8,128)(2,1)S(1)} %get-tuple-element.8) | data formatting | bytes 8388608

commit v4 on v3

--- a/solution.py
+++ b/solution.py
@@ -195,12 +195,13 @@
         for i in range(brows):
             loads[i].wait()
 
-            def norm_pair(t, _, i=i):
-                norms(1 + 2 * i, 1 + t)
-                norms(2 + 2 * i, 1 + t)
+            def norm_group(t, _, i=i):
+                for a in range(2):
+                    for b in range(4):
+                        norms(1 + 2 * i + a, 1 + 4 * t + b)
                 return 0
 
-            lax.fori_loop(0, cols, norm_pair, 0)
+            lax.fori_loop(0, cols // 4, norm_group, 0)
 
         def arrive(bi, bj):
             @pl.when((bi == 0) & has_up)
@@ -297,36 +298,36 @@
 
                 lax.fori_loop(0, 2, one, 0)
 
+        pl.semaphore_wait(barrier, n_gx + n_gy - 2)
+        for off in range(1, n_gx):
+            pl.semaphore_signal(
+                ready, inc=1, device_id={"gx": lax.rem(gx + off, n_gx), "gy": gy}, device_id_type=MESH
+            )
+
+        @pl.when(has_down)
+        def _():
+            for j in v_order:
+                down_copy(j).start()
+
+        @pl.when(has_up)
+        def _():
+            for j in v_order:
+                up_copy(j).start()
+
+        @pl.when(has_right)
+        def _():
+            for i in h_order:
+                right_copy(i).start()
+
+        @pl.when(has_left)
+        def _():
+            for i in h_order:
+                left_copy(i).start()
+
         for slot in range(2):
             node = stage_a(slot, slot)
             for n in range(4):
                 node(n)
-
-        pl.semaphore_wait(barrier, n_gx + n_gy - 2)
-        for off in range(1, n_gx):
-            pl.semaphore_signal(
-                ready, inc=1, device_id={"gx": lax.rem(gx + off, n_gx), "gy": gy}, device_id_type=MESH
-            )
-
-        @pl.when(has_down)
-        def _():
-            for j in v_order:
-                down_copy(j).start()
-
-        @pl.when(has_up)
-        def _():
-            for j in v_order:
-                up_copy(j).start()
-
-        @pl.when(has_right)
-        def _():
-            for i in h_order:
-                right_copy(i).start()
-
-        @pl.when(has_left)
-        def _():
-            for i in h_order:
-                left_copy(i).start()
 
         unroll = 3
 
@@ -375,32 +376,32 @@
         for t in range(len(offs)):
             sum_copy(t).start()
         for t in range(len(offs)):
+            sum_copy(t).wait_send()
+
+        @pl.when(has_down)
+        def _():
+            for j in v_order:
+                down_copy(j).wait_send()
+
+        @pl.when(has_up)
+        def _():
+            for j in v_order:
+                up_copy(j).wait_send()
+
+        @pl.when(has_right)
+        def _():
+            for i in h_order:
+                right_copy(i).wait_send()
+
+        @pl.when(has_left)
+        def _():
+            for i in h_order:
+                left_copy(i).wait_send()
+
+        for t in range(len(offs)):
             sum_copy(t).wait_recv()
         pairs = float(rows * n_gx * cols * n_gy * 256 * 256)
         stein_ref[0, 0] = jnp.sum(ar_all[...]) / pairs
-
-        for t in range(len(offs)):
-            sum_copy(t).wait_send()
-
-        @pl.when(has_down)
-        def _():
-            for j in v_order:
-                down_copy(j).wait_send()
-
-        @pl.when(has_up)
-        def _():
-            for j in v_order:
-                up_copy(j).wait_send()
-
-        @pl.when(has_right)
-        def _():
-            for i in h_order:
-                right_copy(i).wait_send()
-
-        @pl.when(has_left)
-        def _():
-            for i in h_order:
-                left_copy(i).wait_send()
 
 
 def solution(mesh):

time: 39.2 us -> 37.9 us (0.967)
  Pallas kernels: 34.7 us -> 33.4 us
    pallas_call x1, Pallas kernels: 34.7 us -> 33.4 us  [step(): pl.pallas_call(Kernel(n_gx, n_gy, rows, cols), name='svgd', out_shape=(ja...]
where the time goes in v4:
time: 37.9 us; the launch traced here: 37.7 us
  Pallas kernels  33.4 us (88%)
  between operations  2.33 us (6%)
  local copies, waits for them, and re-layouts  2.02 us (5%)
    pallas_call x1, Pallas kernels, step(): pl.pallas_call(Kernel(n_gx, n_gy, rows, cols), name='svgd', out_shape=(ja...  33.4 us
    unnamed x1, local copies, waits for them, and re-layouts  2.02 us

profile of v4, /device:TPU:1, one launch (start us, length us, event | category | flops | bytes accessed | tf_op | source)
XLA Modules:
  0.0 37.7 jit_solution(14838340201880159534)
XLA Ops:
  0.6 33.4 %svgd.1 = (bf16[8,16,64,256]{3,2,1,0:T(8,128)(2,1)S(1)}, f32[1,1]{1,0:T(1,128)}) custom-call(bf16[8,16,64,256]{3,2,1,0:T(8,128)(2,1)} %x_hbm.1, f32[8,16,64]{2,1,0:T(8,128)} %bias_hbm.1, f32[8,16]{1,0:T(8,128)} %spread_hbm.1, bf16[64,64]{1,0:T(8,128)(2,1)} %prec_hbm.1, bf16[64,64]{1,0:T(8,128)(2,1)} %ch_hbm.1, bf16[64,64]{1,0:T(8,128)(2,1)} %cv_hbm.1), custom_call_target="tpu_custom_call" | custom-call | tf_op jit(solution)/shard_map/svgd/pallas_call | solution.py:415
  34.0 2.0 %copy.10 = bf16[8,16,64,256]{3,2,1,0:T(8,128)(2,1)} copy(bf16[8,16,64,256]{3,2,1,0:T(8,128)(2,1)S(1)} %get-tuple-element.8) | data formatting | bytes 8388608

commit v5 on v4

--- a/solution.py
+++ b/solution.py
@@ -67,6 +67,14 @@
         bi = where(on3, (br - 1) * (k3 // 2), bi)
         bj = where(on3, (bc - 1) * (k3 % 2), bj)
         return bi, bj
+
+    def fixed_block(self, k):
+        br, bc = self.brows, self.bcols
+        order = [(i, j) for i in range(1, br - 1) for j in range(1, bc - 1)]
+        order += [(i, j) for j in range(1, bc - 1) for i in (0, br - 1)]
+        order += [(i, j) for i in range(1, br - 1) for j in (0, bc - 1)]
+        order += [(i, j) for i in (0, br - 1) for j in (0, bc - 1)]
+        return order[k]
 
     def __call__(
         self, x_hbm, bias_hbm, spread_hbm, prec_hbm, ch_hbm, cv_hbm, fo, stein_ref,
@@ -142,7 +150,6 @@
             def one(t, _):
                 r, c = row + t // col_count, col + t % col_count
                 xp[r, c] = jnp.zeros((64, 256), BF16)
-                sq[r, c] = jnp.zeros((8, 256), F32)
                 return 0
 
             lax.fori_loop(0, row_count * col_count, one, 0)
@@ -203,30 +210,24 @@
 
             lax.fori_loop(0, cols // 4, norm_group, 0)
 
-        def arrive(bi, bj):
-            @pl.when((bi == 0) & has_up)
-            def _():
-                down_copy(bj).wait_recv()
-                norms(0, 1 + 2 * bj)
-                norms(0, 2 + 2 * bj)
-
-            @pl.when((bi == brows - 1) & has_down)
-            def _():
-                up_copy(bj).wait_recv()
-                norms(rows + 1, 1 + 2 * bj)
-                norms(rows + 1, 2 + 2 * bj)
-
-            @pl.when((bj == 0) & has_left)
-            def _():
-                right_copy(bi).wait_recv()
-                norms(1 + 2 * bi, 0)
-                norms(2 + 2 * bi, 0)
-
-            @pl.when((bj == bcols - 1) & has_right)
-            def _():
-                left_copy(bi).wait_recv()
-                norms(1 + 2 * bi, cols + 1)
-                norms(2 + 2 * bi, cols + 1)
+        def arrivals(first, last):
+            halo = []
+            for k in range(first, last):
+                bi, bj = self.fixed_block(k)
+                if bi == 0:
+                    pl.when(has_up)(lambda bj=bj: down_copy(bj).wait_recv())
+                    halo += [(0, 1 + 2 * bj), (0, 2 + 2 * bj)]
+                if bi == brows - 1:
+                    pl.when(has_down)(lambda bj=bj: up_copy(bj).wait_recv())
+                    halo += [(rows + 1, 1 + 2 * bj), (rows + 1, 2 + 2 * bj)]
+                if bj == 0:
+                    pl.when(has_left)(lambda bi=bi: right_copy(bi).wait_recv())
+                    halo += [(1 + 2 * bi, 0), (2 + 2 * bi, 0)]
+                if bj == bcols - 1:
+                    pl.when(has_right)(lambda bi=bi: left_copy(bi).wait_recv())
+                    halo += [(1 + 2 * bi, cols + 1), (2 + 2 * bi, cols + 1)]
+            for r, c in halo:
+                norms(r, c)
 
         row8 = lax.broadcasted_iota(jnp.int32, (8, 256), 0)
         dims = (((1,), (0,)), ((), ()))
@@ -289,15 +290,6 @@
 
         blocks = brows * bcols
 
-        def pair_arrives(j):
-            @pl.when(2 * j + 1 >= (brows - 2) * (bcols - 2))
-            def _():
-                def one(u, _):
-                    arrive(*self.block_of(2 * j + u))
-                    return 0
-
-                lax.fori_loop(0, 2, one, 0)
-
         pl.semaphore_wait(barrier, n_gx + n_gy - 2)
         for off in range(1, n_gx):
             pl.semaphore_signal(
@@ -330,10 +322,14 @@
                 node(n)
 
         unroll = 3
+        steps = (blocks // 2 - 1) // unroll
+        inner = (brows - 2) * (bcols - 2)
 
         def body(j, _):
-            for u in range(unroll):
-                pair_arrives(unroll * j + u + 1)
+            for step in range(steps):
+                first = 2 * (unroll * step + 1)
+                if first + 2 * unroll > inner:
+                    pl.when(j == step)(functools.partial(arrivals, max(first, inner), first + 2 * unroll))
             for u in range(unroll):
                 p = unroll * j + u
                 for slot in range(2):
@@ -343,7 +339,7 @@
                         ahead(n)
             return 0
 
-        lax.fori_loop(0, (blocks // 2 - 1) // unroll, body, 0)
+        lax.fori_loop(0, steps, body, 0)
         for slot in range(2):
             node = stage_c(blocks - 2 + slot, slot)
             for n in range(4):

time: 37.9 us -> 37.1 us (0.979)
  Pallas kernels: 33.4 us -> 32.5 us
    pallas_call x1, Pallas kernels: 33.4 us -> 32.5 us  [step(): pl.pallas_call(Kernel(n_gx, n_gy, rows, cols), name='svgd', out_shape=(ja...]
where the time goes in v5:
time: 37.1 us; the launch traced here: 36.9 us
  Pallas kernels  32.5 us (88%)
  between operations  2.33 us (6%)
  local copies, waits for them, and re-layouts  2.02 us (5%)
    pallas_call x1, Pallas kernels, step(): pl.pallas_call(Kernel(n_gx, n_gy, rows, cols), name='svgd', out_shape=(ja...  32.5 us
    unnamed x1, local copies, waits for them, and re-layouts  2.02 us

profile of v5, /device:TPU:1, one launch (start us, length us, event | category | flops | bytes accessed | tf_op | source)
XLA Modules:
  0.0 36.9 jit_solution(16923570932653569431)
XLA Ops:
  0.6 32.5 %svgd.1 = (bf16[8,16,64,256]{3,2,1,0:T(8,128)(2,1)S(1)}, f32[1,1]{1,0:T(1,128)}) custom-call(bf16[8,16,64,256]{3,2,1,0:T(8,128)(2,1)} %x_hbm.1, f32[8,16,64]{2,1,0:T(8,128)} %bias_hbm.1, f32[8,16]{1,0:T(8,128)} %spread_hbm.1, bf16[64,64]{1,0:T(8,128)(2,1)} %prec_hbm.1, bf16[64,64]{1,0:T(8,128)(2,1)} %ch_hbm.1, bf16[64,64]{1,0:T(8,128)(2,1)} %cv_hbm.1), custom_call_target="tpu_custom_call" | custom-call | tf_op jit(solution)/shard_map/svgd/pallas_call | solution.py:411
  33.1 2.0 %copy.10 = bf16[8,16,64,256]{3,2,1,0:T(8,128)(2,1)} copy(bf16[8,16,64,256]{3,2,1,0:T(8,128)(2,1)S(1)} %get-tuple-element.8) | data formatting | bytes 8388608

commit v6 on v5

--- a/solution.py
+++ b/solution.py
@@ -109,6 +109,36 @@
                 barrier, inc=1, device_id={"gx": gx, "gy": lax.rem(gy + off, n_gy)}, device_id_type=MESH
             )
 
+        acc[...] = jnp.zeros_like(acc)
+        row = lax.broadcasted_iota(jnp.int32, (8, 256), 0)
+        for slot in range(2):
+            for n in range(4):
+                st[slot, n, 128:144] = jnp.ones((16, 256), BF16)
+        base_r[...] = jnp.where(row < 3, 1.0, 0.0)
+        base_l[...] = jnp.where((row >= 3) & (row < 6), 1.0, 0.0)
+        hot_row = lax.broadcasted_iota(jnp.int32, (48, 256), 0) % 16
+
+        def one_hot(col, _):
+            hot[col] = jnp.where(hot_row == col, 1.0, 0.0).astype(BF16)
+            return 0
+
+        lax.fori_loop(0, cols, one_hot, 0)
+
+        def clear(row, row_count, col, col_count):
+            def one(t, _):
+                r, c = row + t // col_count, col + t % col_count
+                xp[r, c] = jnp.zeros((64, 256), BF16)
+                return 0
+
+            lax.fori_loop(0, row_count * col_count, one, 0)
+
+        has_up, has_down = gx > 0, gx < n_gx - 1
+        has_left, has_right = gy > 0, gy < n_gy - 1
+        pl.when(jnp.logical_not(has_up))(lambda: clear(0, 1, 1, cols))
+        pl.when(jnp.logical_not(has_down))(lambda: clear(rows + 1, 1, 1, cols))
+        pl.when(jnp.logical_not(has_left))(lambda: clear(1, rows, 0, 1))
+        pl.when(jnp.logical_not(has_right))(lambda: clear(1, rows, cols + 1, 1))
+
         for copy in smalls:
             copy.wait()
         minus_a = (-(prec_ref[...].astype(F32))).astype(BF16)
@@ -131,35 +161,6 @@
             tail_t = tail.T
             whb[r, 0] = jnp.concatenate([h_t, tail_t], axis=1)
             whb[r, 1] = jnp.concatenate([h_mat, tail_t], axis=1)
-        acc[...] = jnp.zeros_like(acc)
-        row = lax.broadcasted_iota(jnp.int32, (8, 256), 0)
-        for slot in range(2):
-            for n in range(4):
-                st[slot, n, 128:144] = jnp.ones((16, 256), BF16)
-        base_r[...] = jnp.where(row < 3, 1.0, 0.0)
-        base_l[...] = jnp.where((row >= 3) & (row < 6), 1.0, 0.0)
-        hot_row = lax.broadcasted_iota(jnp.int32, (48, 256), 0) % 16
-
-        def one_hot(col, _):
-            hot[col] = jnp.where(hot_row == col, 1.0, 0.0).astype(BF16)
-            return 0
-
-        lax.fori_loop(0, cols, one_hot, 0)
-
-        def clear(row, row_count, col, col_count):
-            def one(t, _):
-                r, c = row + t // col_count, col + t % col_count
-                xp[r, c] = jnp.zeros((64, 256), BF16)
-                return 0
-
-            lax.fori_loop(0, row_count * col_count, one, 0)
-
-        has_up, has_down = gx > 0, gx < n_gx - 1
-        has_left, has_right = gy > 0, gy < n_gy - 1
-        pl.when(jnp.logical_not(has_up))(lambda: clear(0, 1, 1, cols))
-        pl.when(jnp.logical_not(has_down))(lambda: clear(rows + 1, 1, 1, cols))
-        pl.when(jnp.logical_not(has_left))(lambda: clear(1, rows, 0, 1))
-        pl.when(jnp.logical_not(has_right))(lambda: clear(1, rows, cols + 1, 1))
 
         def down_copy(j):
             return pltpu.make_async_remote_copy(

time: 37.1 us -> 36.9 us (level)
  no operation moved by 1% of the time
where the time goes in v6:
time: 36.9 us; the launch traced here: 36.7 us
  Pallas kernels  32.4 us (88%)
  between operations  2.33 us (6%)
  local copies, waits for them, and re-layouts  2.02 us (5%)
    pallas_call x1, Pallas kernels, step(): pl.pallas_call(Kernel(n_gx, n_gy, rows, cols), name='svgd', out_shape=(ja...  32.4 us
    unnamed x1, local copies, waits for them, and re-layouts  2.02 us

profile of v6, /device:TPU:1, one launch (start us, length us, event | category | flops | bytes accessed | tf_op | source)
XLA Modules:
  0.0 36.7 jit_solution(2641450276903780726)
XLA Ops:
  0.6 32.4 %svgd.1 = (bf16[8,16,64,256]{3,2,1,0:T(8,128)(2,1)S(1)}, f32[1,1]{1,0:T(1,128)}) custom-call(bf16[8,16,64,256]{3,2,1,0:T(8,128)(2,1)} %x_hbm.1, f32[8,16,64]{2,1,0:T(8,128)} %bias_hbm.1, f32[8,16]{1,0:T(8,128)} %spread_hbm.1, bf16[64,64]{1,0:T(8,128)(2,1)} %prec_hbm.1, bf16[64,64]{1,0:T(8,128)(2,1)} %ch_hbm.1, bf16[64,64]{1,0:T(8,128)(2,1)} %cv_hbm.1), custom_call_target="tpu_custom_call" | custom-call | tf_op jit(solution)/shard_map/svgd/pallas_call | solution.py:412
  33.0 2.0 %copy.10 = bf16[8,16,64,256]{3,2,1,0:T(8,128)(2,1)} copy(bf16[8,16,64,256]{3,2,1,0:T(8,128)(2,1)S(1)} %get-tuple-element.8) | data formatting | bytes 8388608
